TPU v7x, 256 devices: a whole 4x4x8 slice. The times are simulated.
256 devices in a mesh: band: 128 (over z, y, x), ch: 2 (over core).
Axes of the slice: x: 4, y: 4, z: 8, core: 2. Of those that a mesh axis runs over, the one named last changes fastest.
Arguments:
- grid_field: bfloat16 [100, 2097152], P(None, 'band'), may hold values from -6 to 6
- band_points: int32 [128], P('band'), may hold values from 8192 to 16384
- block_ids: int32 [128, 16], P('band'), may hold values from 0 to 4095, as said below
- block_count: int32 [128], P('band'), may hold values from 8 to 16
- block_weight: bfloat16 [128, 16, 256, 512], P('band'), may hold values from 0 to 0.039794922
- embed_weight: bfloat16 [100, 1024], P(None, 'ch'), may hold values from -0.3125 to 0.3125
- edge_src: int32 [655360], P('band'), may hold values from 0 to 32767, as said below
- edge_dst: int32 [655360], P('band'), may hold values from 0 to 32767, as said below
- edge_in_weight: bfloat16 [2, 1024, 1024], P(None, None, 'ch'), may hold values from -0.1875 to 0.1875
- edge_out_weight: bfloat16 [1024, 1024], P('ch'), may hold values from -0.0625 to 0.0625
- node_in_weight: bfloat16 [2, 1024, 1024], P(None, None, 'ch'), may hold values from -0.125 to 0.125
- node_out_weight: bfloat16 [1024, 1024], P('ch'), may hold values from -0.1875 to 0.1875
Outputs:
- node_state: bfloat16 [32768, 1024], P('band', 'ch')
Inputs may be any that keep to these rules, and one draw needn't show every extreme that they name: For band b, block_ids[b, k] * 512 lies from max(b * 16384 - 16384 // 2, 0) to min((b + 1) * 16384 + 16384 // 2, 2097152) - 512; both ends are named by every band; ids may repeat. `edge_src`: edge e belongs to band b = e // 5120; its source node lies in bands b - 1 to b + 1 of the mesh. `edge_dst`: edge e ends at a node of its band b = e // 5120.
All inputs are finite; a program needn't handle non-finite values.
Results may differ from a plain program's by a relative error of at most 0.015.
Values may be sent and summed in bfloat16 or wider, within the bound.
A program may use at most 64 MiB of HBM per device.

v0:
```python
import functools

import jax
import jax.numpy as jnp
from jax import lax
from jax.experimental import pallas as pl
from jax.experimental.pallas import tpu as pltpu
from jax.sharding import PartitionSpec as P

MESH = pl.DeviceIdType.MESH
F32 = jnp.float32
BF16 = jnp.bfloat16
VMEM = pl.BlockSpec(memory_space=pltpu.VMEM)
SMEM = pl.BlockSpec(memory_space=pltpu.SMEM)
ANY = pl.BlockSpec(memory_space=pl.ANY)
HBM = pl.BlockSpec(memory_space=pltpu.HBM)
SMALL = 12 * 1024 * 1024
LARGE = 40 * 1024 * 1024
UNROLL = 2


def buckets(most):
    pairs = [(4, 6), (5, 7), (7, 9)]
    return [p for p in pairs if max(p) < most] + [(most, most)]


def meta_kernel(n, slots, sub, block_len, sizes, ids, count, live, out, choice, row, rows, send, recv):
    b = lax.axis_index("band")
    c = lax.axis_index("ch")
    half = sub // 2
    row[:, :slots] = ids[...]
    row[:, slots:2 * slots] = jnp.full((1, slots), count[0], jnp.int32)
    row[:, 2 * slots:3 * slots] = jnp.full((1, slots), live[0], jnp.int32)
    row[:, 3 * slots:] = jnp.zeros((1, row.shape[1] - 3 * slots), jnp.int32)
    barrier = pltpu.get_barrier_semaphore()

    def greet(d, carry):
        pl.semaphore_signal(barrier, inc=1, device_id=(lax.rem(b + d, n), c), device_id_type=MESH)
        return carry

    lax.fori_loop(1, n, greet, 0)
    pl.semaphore_wait(barrier, n - 1)

    def copy(d):
        return pltpu.make_async_remote_copy(
            src_ref=row, dst_ref=rows.at[b], send_sem=send.at[d], recv_sem=recv.at[d],
            device_id=(lax.rem(b + d, n), c), device_id_type=MESH,
        )

    def begin(d, carry):
        copy(d).start()
        return carry

    def arrive(d, carry):
        pltpu.make_async_remote_copy(
            src_ref=row, dst_ref=rows.at[lax.rem(b + n - d, n)], send_sem=send.at[d], recv_sem=recv.at[d],
            device_id=(lax.rem(b + d, n), c), device_id_type=MESH,
        ).wait()
        return carry

    lax.fori_loop(1, n, begin, 0)
    rows[b] = row[...]
    lax.fori_loop(1, n, arrive, 0)
    out[...] = rows[...]
    every = rows[:, 0, :]
    named, most, points = every[:, :slots], every[:, slots:2 * slots], every[:, 2 * slots:2 * slots + 1]
    below = jnp.concatenate([points[:1], points[:-1]], axis=0)
    above = jnp.concatenate([points[1:], points[-1:]], axis=0)
    bands = lax.broadcasted_iota(jnp.int32, (n, 1), 0)
    rel = named - bands * sub + half
    rel = jnp.where(lax.broadcasted_iota(jnp.int32, (n, slots), 1) < most, rel, -1)
    counts = []
    for side in range(2):
        total = jnp.zeros((n, 1), F32)
        for i in range(half):
            spot = i if side == 0 else half + sub + i
            hit = jnp.max(jnp.where(rel == spot, 1.0, 0.0), axis=1, keepdims=True)
            alive = (half + i) * block_len < below if side == 0 else i * block_len < above
            total += jnp.where(alive, hit, 0.0)
        counts.append(jnp.max(total, axis=0, keepdims=True))
    pick = jnp.zeros((1, 1), jnp.int32)
    for low, high in sizes[:-1]:
        pick += jnp.where((counts[0] > low) | (counts[1] > high), 1, 0)
    choice[...] = jnp.broadcast_to(pick, choice.shape)


def pack_kernel(n, slots, sub, block_len, meta, grid_ref, out_ref, kind, index, limit, need, rank, mine, place, sem):
    b = lax.axis_index("band")
    core = lax.axis_index("ch")
    half = sub // 2
    width = block_len // 2

    def mark(side, band, owner, flags, ranks, active):
        for i in range(half):
            flags[side, i] = 0
        for k in range(slots):
            rel = meta[band, 0, k] - band * sub + half
            i = rel if side == 0 else rel - half - sub
            inner = rel + half if side == 0 else i
            good = (i >= 0) & (i < half) & (k < meta[band, 0, slots])
            good &= (inner * block_len < meta[owner, 0, 2 * slots]) & active
            i = jnp.clip(i, 0, half - 1)
            flags[side, i] = flags[side, i] | good.astype(jnp.int32)
        run = jnp.int32(0)
        for i in range(half):
            ranks[side, i] = run
            run += flags[side, i]

    up, down = jnp.minimum(b + 1, n - 1), jnp.maximum(b - 1, 0)

    def copy(side, i):
        block = half + i if side == 0 else i
        start = pl.multiple_of((block * 2 + core) * width, width)
        return pltpu.make_async_copy(
            grid_ref.at[:, pl.ds(start, width)], out_ref.at[side, rank[side, i]], sem.at[side, i]
        )

    def each(begin, side):
        for i in range(half):
            @pl.when(need[side, i] > 0)
            def _():
                if begin:
                    copy(side, i).start()
                else:
                    copy(side, i).wait()

    mark(0, up, b, need, rank, b < n - 1)
    each(True, 0)
    mark(1, down, b, need, rank, b > 0)
    each(True, 1)
    mark(0, b, down, mine, place, b > 0)
    mark(1, b, up, mine, place, b < n - 1)
    for k in range(slots):
        rel = meta[b, 0, k] - b * sub + half
        is_low, is_high = rel < half, rel >= half + sub
        side = is_high.astype(jnp.int32)
        i = jnp.clip(jnp.where(is_low, rel, rel - half - sub), 0, half - 1)
        used = k < meta[b, 0, slots]
        outside = is_low | is_high
        far = outside & used & (mine[side, i] > 0)
        owner = jnp.where(is_low, down, jnp.where(is_high, up, b))
        inner = jnp.where(is_low, rel + half, jnp.where(is_high, rel - half - sub, rel - half))
        span = jnp.clip(meta[owner, 0, 2 * slots] - inner * block_len, 0, block_len)
        kind[k] = jnp.where(far, 1 + side, 0)
        local = jnp.clip(rel - half, 0, sub - 1)
        index[k] = jnp.where(far, place[side, i], local)
        limit[k] = jnp.where(used & (far | ~outside), span, 0)
    each(False, 0)
    each(False, 1)


def silu(v):
    return (0.5 * v) * (1.0 + jnp.tanh(0.5 * v))


def layer_kernel(
    n, low, high, chunk, kind, index, limit, pk, grid_h, w_h, emb_h, eo_h, win_h, nin_h, nout_h, src, dst, out,
    rlow, rhigh, loc, wts, blk, part, other, ext, emb, emb_o, eo, eo_o, win, nin, nout,
    init, table, acc, direct, agg, agg_o, give, take, wsem, gsem, lsem, send, recv,
):
    b = lax.axis_index("band")
    c = lax.axis_index("ch")
    sub, channels, width = loc.shape
    slots = w_h.shape[0]
    nodes = part.shape[0]
    half = emb.shape[1]
    up, down = jnp.minimum(b + 1, n - 1), jnp.maximum(b - 1, 0)
    has_up, has_down = b < n - 1, b > 0
    above, below, partner = (up, c), (down, c), (b, 1 - c)
    barrier = pltpu.get_barrier_semaphore()
    pl.semaphore_signal(barrier, inc=1, device_id=partner, device_id_type=MESH)

    @pl.when(has_up)
    def _():
        pl.semaphore_signal(barrier, inc=1, device_id=above, device_id_type=MESH)

    @pl.when(has_down)
    def _():
        pl.semaphore_signal(barrier, inc=1, device_id=below, device_id_type=MESH)

    pl.semaphore_wait(barrier, 1 + has_up.astype(jnp.int32) + has_down.astype(jnp.int32))

    def remote(source, target, k, device):
        return pltpu.make_async_remote_copy(
            src_ref=source, dst_ref=target, send_sem=send.at[k], recv_sem=recv.at[k],
            device_id=device, device_id_type=MESH,
        )

    def neighbours(fwd, bwd):
        def begin():
            pl.when(has_up)(fwd.start)
            pl.when(has_down)(bwd.start)

        def end():
            @pl.when(has_up)
            def _():
                fwd.wait_send()
                bwd.wait_recv()

            @pl.when(has_down)
            def _():
                bwd.wait_send()
                fwd.wait_recv()

        return begin, end

    blocks_begin, blocks_end = neighbours(
        remote(pk.at[0, pl.ds(0, low)], rlow, 0, above), remote(pk.at[1, pl.ds(0, high)], rhigh, 1, below)
    )
    blocks_begin()
    weights = [remote(emb_h, emb_o, 2, partner), remote(eo_h, eo_o, 3, partner)]
    for one in weights:
        one.start()
    off = pl.multiple_of(c * width, width)
    wcopies = [
        pltpu.make_async_copy(w_h.at[k, :, pl.ds(off, width)], wts.at[:, pl.ds(k * width, width)], wsem.at[k])
        for k in range(slots)
    ]
    gcopies = [
        pltpu.make_async_copy(
            grid_h.at[:, pl.ds(pl.multiple_of((2 * i + c) * width, width), width)], loc.at[i], gsem.at[i]
        )
        for i in range(sub)
    ]
    local = [
        pltpu.make_async_copy(x, y, lsem.at[i])
        for i, (x, y) in enumerate(
            [(emb_h, emb), (win_h, win), (eo_h, eo), (nin_h, nin), (nout_h, nout)]
        )
    ]
    for one in wcopies + gcopies + local:
        one.start()

    @pl.when(b == 0)
    def _():
        rlow[...] = jnp.zeros_like(rlow)
        ext[0] = jnp.zeros((nodes, channels), BF16)

    @pl.when(b == n - 1)
    def _():
        rhigh[...] = jnp.zeros_like(rhigh)
        ext[2] = jnp.zeros((nodes, channels), BF16)

    for one in wcopies + gcopies + local + weights:
        one.wait()
    blocks_end()

    column = lax.broadcasted_iota(jnp.int32, (channels, width), 1) + c * width
    for k in range(slots):
        which, i = kind[k], index[k]
        block = jnp.where(which == 1, rlow[jnp.clip(i, 0, low - 1)], loc[i])
        block = jnp.where(which == 2, rhigh[jnp.clip(i, 0, high - 1)], block)
        blk[:, k * width:(k + 1) * width] = jnp.where(column < limit[k], block, jnp.zeros_like(block))
    part[...] = lax.dot_general(wts[...], blk[...], (((1,), (1,)), ((), ())), preferred_element_type=F32)
    swap = remote(part, other, 4, partner)
    swap.start()
    swap.wait()
    ext[1] = (part[...] + other[...]).astype(BF16)
    rows_begin, rows_end = neighbours(remote(ext.at[1], ext.at[0], 5, above), remote(ext.at[1], ext.at[2], 6, below))
    rows_begin()

    mine = pl.ds(pl.multiple_of(c * half, half), half)
    theirs = pl.ds(pl.multiple_of((1 - c) * half, half), half)

    def project(i):
        rem = ext[i]
        init[i, :, mine] = jnp.dot(rem, emb[...], preferred_element_type=F32).astype(BF16)
        init[i, :, theirs] = jnp.dot(rem, emb_o[...], preferred_element_type=F32).astype(BF16)
        source = jnp.dot(init[i], win[0], preferred_element_type=F32)
        table[:, i * nodes:(i + 1) * nodes] = source.T.astype(BF16)

    project(1)
    target = jnp.dot(init[1], win[1], preferred_element_type=F32)
    table[:, 3 * nodes:] = target.T.astype(BF16)
    direct[...] = jnp.dot(init[1], nin[0], preferred_element_type=F32)
    acc[...] = jnp.zeros_like(acc)
    rows_end()
    project(0)
    project(2)

    def step(i, carry):
        cols = pl.ds(pl.multiple_of(i * chunk, chunk), chunk)
        s = src[:, cols] - (b - 1) * nodes
        d = dst[:, cols] - b * nodes
        from_src = lax.broadcasted_iota(jnp.int32, (3 * nodes, chunk), 0) == s
        from_dst = lax.broadcasted_iota(jnp.int32, (nodes, chunk), 0) == d
        hot_src = jnp.where(from_src, 1.0, 0.0).astype(BF16)
        hot_dst = jnp.where(from_dst, 1.0, 0.0).astype(BF16)
        pre = jnp.dot(table[...], jnp.concatenate([hot_src, hot_dst], axis=0), preferred_element_type=F32)
        hidden = silu(pre).astype(BF16)
        acc[...] += lax.dot_general(hot_dst, hidden, (((1,), (1,)), ((), ())), preferred_element_type=F32)
        return carry

    lax.fori_loop(0, src.shape[1] // chunk, step, 0, unroll=UNROLL)
    agg[...] = acc[...].astype(BF16)

    swap = remote(agg, agg_o, 7, partner)
    swap.start()
    own = jnp.dot(agg[...], eo[...], preferred_element_type=F32)
    swap.wait()
    total = (own + jnp.dot(agg_o[...], eo_o[...], preferred_element_type=F32)).astype(BF16)
    update = silu(direct[...] + jnp.dot(total, nin[1], preferred_element_type=F32)).astype(BF16)
    give[...] = jnp.dot(update, nout[:, theirs], preferred_element_type=F32).astype(BF16)
    last = remote(give, take, 8, partner)
    last.start()
    kept = init[1, :, mine].astype(F32) + jnp.dot(update, nout[:, mine], preferred_element_type=F32)
    last.wait()
    out[...] = (kept + take[...].astype(F32)).astype(BF16)


def on_device(
    grid_field, band_points, block_ids, block_count, block_weight, embed_weight,
    edge_src, edge_dst, edge_in_weight, edge_out_weight, node_in_weight, node_out_weight,
):
    n = lax.axis_size("band")
    channels, points = grid_field.shape
    slots, nodes, block_len = block_weight.shape[1:]
    sub = points // block_len
    half = sub // 2
    width = block_len // 2
    hid = embed_weight.shape[1]
    params = lambda limit, **kw: pltpu.CompilerParams(vmem_limit_bytes=limit, **kw)

    sizes = buckets(half)
    meta, choice = pl.pallas_call(
        functools.partial(meta_kernel, n, slots, sub, block_len, sizes),
        out_shape=(
            jax.ShapeDtypeStruct((n, 1, 128), jnp.int32),
            jax.ShapeDtypeStruct((1, 128), jnp.int32),
        ),
        in_specs=[VMEM, SMEM, SMEM], out_specs=(VMEM, VMEM),
        scratch_shapes=[
            pltpu.VMEM((1, 128), jnp.int32),
            pltpu.VMEM((n, 1, 128), jnp.int32),
            pltpu.SemaphoreType.DMA((n,)), pltpu.SemaphoreType.DMA((n,)),
        ],
        compiler_params=params(SMALL, collective_id=len(sizes) + 2, has_side_effects=True),
    )(block_ids, block_count, band_points)

    slot_shape = (2, half, channels, width)
    lists = jax.ShapeDtypeStruct((slots,), jnp.int32)
    table = pltpu.SMEM((2, half), jnp.int32)
    packed, kind, index, limit = pl.pallas_call(
        functools.partial(pack_kernel, n, slots, sub, block_len),
        out_shape=(jax.ShapeDtypeStruct(slot_shape, BF16), lists, lists, lists),
        in_specs=[SMEM, HBM], out_specs=(VMEM, SMEM, SMEM, SMEM),
        scratch_shapes=[table] * 4 + [pltpu.SemaphoreType.DMA((2, half))],
        compiler_params=params(SMALL),
    )(meta, grid_field)

    edges = edge_src.shape[0]
    chunk = max(c for c in (512, 256, 128) if edges % c == 0)

    def layer(i, low, high, *args):
        bf = lambda *shape: pltpu.VMEM(shape, BF16)
        f32 = lambda *shape: pltpu.VMEM(shape, F32)
        return pl.pallas_call(
            functools.partial(layer_kernel, n, low, high, chunk),
            out_shape=jax.ShapeDtypeStruct((nodes, hid), BF16),
            in_specs=[SMEM] * 3 + [ANY] + [HBM] * 7 + [VMEM] * 2, out_specs=VMEM,
            scratch_shapes=[
                bf(low, channels, width), bf(high, channels, width), bf(sub, channels, width),
                bf(nodes, slots * width), bf(channels, slots * width),
                f32(nodes, channels), f32(nodes, channels), bf(3, nodes, channels),
                bf(channels, hid), bf(channels, hid), bf(hid, 2 * hid), bf(hid, 2 * hid),
                bf(2, 2 * hid, hid), bf(2, 2 * hid, hid), bf(hid, 2 * hid),
                bf(3, nodes, 2 * hid), bf(hid, 4 * nodes), f32(nodes, hid), f32(nodes, hid),
                bf(nodes, hid), bf(nodes, hid), bf(nodes, hid), bf(nodes, hid),
                pltpu.SemaphoreType.DMA((slots,)), pltpu.SemaphoreType.DMA((sub,)), pltpu.SemaphoreType.DMA((5,)),
                pltpu.SemaphoreType.DMA((9,)), pltpu.SemaphoreType.DMA((9,)),
            ],
            compiler_params=params(LARGE, collective_id=i, has_side_effects=True),
        )(*args)

    return lax.switch(
        choice[0, 0],
        [functools.partial(layer, i, low, high) for i, (low, high) in enumerate(sizes)],
        kind, index, limit, packed, grid_field, block_weight.reshape(block_weight.shape[1:]), embed_weight, edge_out_weight,
        edge_in_weight, node_in_weight, node_out_weight, edge_src.reshape(1, -1), edge_dst.reshape(1, -1),
    )


def solution(mesh):
    return jax.shard_map(
        on_device,
        mesh=mesh,
        in_specs=(
            P(None, "band"), P("band"), P("band", None), P("band"),
            P("band", None, None, None), P(None, "ch"), P("band"), P("band"),
            P(None, None, "ch"), P("ch", None), P(None, None, "ch"), P("ch", None),
        ),
        out_specs=P("band", "ch"),
        check_vma=False,
    )
```

profile of v0, /device:TPU:33, one launch (start us, length us, event | category | flops | bytes accessed | tf_op | source)
XLA Modules:
  0.0 69.3 jit_solution(8133999101373951543)
XLA Ops:
  1.3 0.0 copy-start
  1.3 0.6 copy-done
  2.0 0.0 copy-start.1
  2.0 0.0 copy-start.2
  2.0 0.0 copy-start.3
  2.0 19.8 %shard_map.122 = (s32[128,1,128]{2,1,0:T(1,128)S(1)}, s32[1,128]{1,0:T(1,128)S(1)}) custom-call(s32[1,16]{1,0:T(1,128)S(1)} %copy-done, s32[1]{0:T(128)S(6)} %copy.23.count, s32[1]{0:T(128)S(6)} %copy.22.live), custom_call_target="tpu_custom_call" | custom-call | tf_op jit(solution)/shard_map/pallas_call | solution.py:325
  21.8 4.4 %shard_map.123 = (bf16[2,16,100,256]{3,2,1,0:T(8,128)(2,1)S(1)}, s32[16]{0:T(128)S(1)}, s32[16]{0:T(128)S(1)}, s32[16]{0:T(128)S(1)}) custom-call(s32[128,1,128]{2,1,0:T(1,128)S(1)} %get-tuple-element.173.meta, bf16[100,16384]{1,0:T(8,128)(2,1)} %grid_ref.1), custom_call_target="tpu_custom_call" | custom-call | tf_op jit(solution)/shard_map/pallas_call | solution.py:343
  26.2 0.0 copy-done.1
  26.2 0.0 copy-done.2
  26.2 0.0 copy-done.3
  26.2 42.4 %conditional.1 = (bf16[256,512]{1,0:T(8,128)(2,1)S(1)}) conditional(s32[]{:T(128)} %bitcast, (s32[16]{0:T(128)S(1)}, s32[16]{0:T(128)S(1)}, s32[16]{0:T(128)S(1)}, bf16[2,16,100,256]{3,2,1,0:T(8,128)(2,1)S(1)}, bf16[100,16384]{1,0:T(8,128)(2,1)S(1)}, /*index=5*/bf16[16,256,512]{2,1,0:T(8,128)(2,1)}, ...), branch_computations={%region_0.0_spmd, %region_1.0_spmd, %region_2.0_spmd, %region_3.0_... | conditional | bytes 8 | solution.py:375
  26.5 41.8 %branch_2_fun.1 = bf16[256,512]{1,0:T(8,128)(2,1)S(1)} custom-call(s32[16]{0:T(128)S(1)} %get-tuple-element.140.kind, s32[16]{0:T(128)S(1)} %get-tuple-element.141.index, s32[16]{0:T(128)S(1)} %get-tuple-element.142.limit, bf16[2,16,100,256]{3,2,1,0:T(8,128)(2,1)S(1)} %get-tuple-element.143.pk, bf16[100,16384]{1,0:T(8,128)(2,1)S(1)} %get-tuple-element.144.grid_h, ...), custom_call_target="tpu_custom_call" | custom-call | tf_op jit(solution)/shard_map/cond/branch_2_fun/pallas_call | solution.py:357
  68.6 0.7 %copy.24 = bf16[256,512]{1,0:T(8,128)(2,1)} copy(bf16[256,512]{1,0:T(8,128)(2,1)S(1)} %get-tuple-element.178) | data formatting | bytes 524288
Async XLA Ops:
  1.3 0.7 copy-start
  2.0 24.2 %copy-start.1 = (bf16[100,16384]{1,0:T(8,128)(2,1)S(1)}, bf16[100,16384]{1,0:T(8,128)(2,1)}, u32[]{:S(2)}) copy-start(bf16[100,16384]{1,0:T(8,128)(2,1)} %grid_ref.1) | copy-start | bytes 9830404
  2.0 24.2 %copy-start.2 = (s32[5120]{0:T(1024)S(1)}, s32[5120]{0:T(1024)}, u32[]{:S(2)}) copy-start(s32[5120]{0:T(1024)} %param.22) | copy-start | bytes 61444
  2.0 24.2 %copy-start.3 = (s32[5120]{0:T(1024)S(1)}, s32[5120]{0:T(1024)}, u32[]{:S(2)}) copy-start(s32[5120]{0:T(1024)} %param.23) | copy-start | bytes 61444
where the time goes:
time: 69.5 us; the launch traced here: 69.3 us
  Pallas kernels  66 us (95%)
  between operations  1.39 us (2%)
  local copies, waits for them, and re-layouts  1.36 us (2%)
    pallas_call x1, Pallas kernels, layer(): pl.pallas_call(functools.partial(layer_kernel, n, low, high, chunk), out_...  41.8 us
    pallas_call x1, Pallas kernels, on_device(): pl.pallas_call(functools.partial(meta_kernel, n, slots, sub, block_len, s...  19.8 us
    pallas_call x1, Pallas kernels, on_device(): pl.pallas_call(functools.partial(pack_kernel, n, slots, sub, block_len),...  4.37 us

commit v1 on v0

v1 whole, which is shorter than its diff:
```python
import functools

import jax
import jax.numpy as jnp
from jax import lax
from jax.experimental import pallas as pl
from jax.experimental.pallas import tpu as pltpu
from jax.sharding import PartitionSpec as P

MESH = pl.DeviceIdType.MESH
F32 = jnp.float32
BF16 = jnp.bfloat16
VMEM = pl.BlockSpec(memory_space=pltpu.VMEM)
SMEM = pl.BlockSpec(memory_space=pltpu.SMEM)
HBM = pl.BlockSpec(memory_space=pltpu.HBM)
LARGE = 48 * 1024 * 1024
CHUNK = 512
PAD = 128


def nt(x, y):
    return lax.dot_general(x, y, (((1,), (1,)), ((), ())), preferred_element_type=F32)


def mm(x, y):
    return jnp.dot(x, y, preferred_element_type=F32)


def silu_of_half(v):
    return v + v * jnp.tanh(v)


def layer_kernel(
    n, ids, count, live, grid_h, w_h, emb_h, eo_h, win_h, nin_h, nout_h, src_h, dst_h, out,
    pool, wts, emb, embp, eo, win, nin, nout, nout_o, src, dst,
    mt, dmix, pmix, hs, hd, part, other, ext, near, gown, gdst, acc, agg, agg_o, upd, upd_o,
    wsem, gsem, lsem, send, recv,
):
    b = lax.axis_index("band")
    c = lax.axis_index("ch")
    slots, nodes, block_len = w_h.shape
    width = block_len // 2
    channels = grid_h.shape[0]
    sub = grid_h.shape[1] // block_len
    half = sub // 2
    cols = emb_h.shape[1]
    hid = 2 * cols
    mine_e = src.shape[1]
    chunks = mine_e // CHUNK
    dead = 2 * sub
    up, down = jnp.minimum(b + 1, n - 1), jnp.maximum(b - 1, 0)
    has_up, has_down = b < n - 1, b > 0
    above, below, partner = (up, c), (down, c), (b, 1 - c)

    ext[...] = jnp.zeros_like(ext)
    barrier = pltpu.get_barrier_semaphore()
    pl.semaphore_signal(barrier, inc=1, device_id=partner, device_id_type=MESH)

    @pl.when(has_up)
    def _():
        pl.semaphore_signal(barrier, inc=1, device_id=above, device_id_type=MESH)

    @pl.when(has_down)
    def _():
        pl.semaphore_signal(barrier, inc=1, device_id=below, device_id_type=MESH)

    off = pl.multiple_of(c * width, width)
    gcopies = [
        pltpu.make_async_copy(
            grid_h.at[:, pl.ds(pl.multiple_of((2 * i + c) * width, width), width)], pool.at[half + i], gsem.at[i]
        )
        for i in range(sub)
    ]
    wcopies = [
        pltpu.make_async_copy(w_h.at[k, :, pl.ds(off, width)], wts.at[:, pl.ds(k * width, width)], wsem.at[k])
        for k in range(slots)
    ]
    mine = pl.ds(pl.multiple_of(c * cols, cols), cols)
    theirs = pl.ds(pl.multiple_of((1 - c) * cols, cols), cols)
    edges = pl.ds(pl.multiple_of(c * mine_e, mine_e), mine_e)
    local = [
        pltpu.make_async_copy(x, y, lsem.at[i])
        for i, (x, y) in enumerate(
            [(emb_h, emb.at[c]), (win_h, win), (eo_h, eo.at[c]), (nin_h, nin), (nout_h.at[:, mine], nout),
             (src_h.at[:, edges], src), (dst_h.at[:, edges], dst)]
        )
    ]
    for one in gcopies[half:] + gcopies[:half] + local + wcopies:
        one.start()

    def remote(source, target, k, device):
        return pltpu.make_async_remote_copy(
            src_ref=source, dst_ref=target, send_sem=send.at[k], recv_sem=recv.at[k],
            device_id=device, device_id_type=MESH,
        )

    def neighbours(fwd, bwd):
        def end():
            @pl.when(has_up)
            def _():
                fwd.wait_send()
                bwd.wait_recv()

            @pl.when(has_down)
            def _():
                bwd.wait_send()
                fwd.wait_recv()

        return (lambda: pl.when(has_up)(fwd.start)), (lambda: pl.when(has_down)(bwd.start)), end

    halo_up, halo_down, halo_end = neighbours(
        remote(pool.at[pl.ds(sub, half)], pool.at[pl.ds(0, half)], 0, above),
        remote(pool.at[pl.ds(half, half)], pool.at[pl.ds(half + sub, half)], 1, below),
    )
    rows_up, rows_down, rows_end = neighbours(
        remote(ext.at[1], ext.at[0], 7, above), remote(ext.at[1], ext.at[2], 8, below)
    )
    weights = [
        remote(emb_h, emb.at[c], 2, partner), remote(eo_h, eo.at[c], 3, partner),
        remote(nout_h.at[:, theirs], nout_o, 4, partner),
    ]

    for one in gcopies:
        one.wait()
    column = lax.broadcasted_iota(jnp.int32, (channels, width), 1) + c * width
    for i in range(half, sub):
        block = pool[half + i]
        pool[half + i] = jnp.where(column < live[0] - i * block_len, block, jnp.zeros_like(block))
    pool[dead] = jnp.zeros((channels, width), BF16)

    @pl.when(b == 0)
    def _():
        pool[0:half] = jnp.zeros((half, channels, width), BF16)

    @pl.when(b == n - 1)
    def _():
        pool[half + sub:dead] = jnp.zeros((half, channels, width), BF16)

    pl.semaphore_wait(barrier, 1 + has_up.astype(jnp.int32) + has_down.astype(jnp.int32))
    halo_up()
    halo_down()
    for one in weights:
        one.start()

    for one in local + weights:
        one.wait()
    embp[...] = jnp.zeros_like(embp)
    embp[0:channels, 0:cols] = emb[0]
    embp[0:channels, cols:hid] = emb[1]
    for i in range(2):
        mixed = mm(embp[...], win[i]) * 0.5
        mt[mine, i * PAD:(i + 1) * PAD] = mixed.T.astype(BF16)
    share = remote(mt.at[mine], mt.at[mine], 5, partner)
    share.start()
    dmix[...] = mm(embp[...], nin[0]).astype(BF16)
    for i in range(2):
        pmix[i * cols:(i + 1) * cols, :] = mm(eo[i], nin[1]).astype(BF16)

    def hot(i, carry):
        at = pl.ds(pl.multiple_of(i * CHUNK, CHUNK), CHUNK)
        s = src[:, at] - (b - 1) * nodes
        s = jnp.where(s < nodes, s, jnp.where(s < 2 * nodes, s + nodes, s - nodes))
        d = dst[:, at] - b * nodes
        hs[:, at] = jnp.where(lax.broadcasted_iota(jnp.int32, (3 * nodes, CHUNK), 0) == s, 1.0, 0.0).astype(BF16)
        hd[:, at] = jnp.where(lax.broadcasted_iota(jnp.int32, (nodes, CHUNK), 0) == d, 1.0, 0.0).astype(BF16)
        return carry

    lax.fori_loop(0, chunks, hot, 0)
    acc[...] = jnp.zeros_like(acc)
    part[...] = jnp.zeros_like(part)
    share.wait()
    for one in wcopies:
        one.wait()
    halo_end()

    picked = []
    for k in range(slots):
        rel = jnp.clip(ids[0, k] - b * sub + half, 0, dead - 1)
        picked.append(pool[jnp.where(k < count[0], rel, dead)])
    part[0:channels, :] = nt(jnp.concatenate(picked, axis=1), wts[...])
    swap = remote(part, other, 6, partner)
    swap.start()
    swap.wait()
    own = (part[...] + other[...]).astype(BF16)
    ext[1] = own
    rows_up()
    rows_down()

    rows = own.astype(F32).T.astype(BF16)
    first = mm(rows, embp[:, mine]).astype(BF16).astype(F32)
    inner = mm(rows, dmix[...])
    gdst[...] = mm(own, hd[...]).astype(BF16)
    gown[...] = mm(own, hs[2 * nodes:, :]).astype(BF16)
    rows_end()
    near[:, 0:nodes] = ext[0]
    near[:, nodes:] = ext[2]

    def step(i, carry):
        at = pl.ds(pl.multiple_of(i * CHUNK, CHUNK), CHUNK)
        gsrc = (mm(near[...], hs[0:2 * nodes, at]) + gown[:, at].astype(F32)).astype(BF16)
        pre = mm(mt[...], jnp.concatenate([gsrc, gdst[:, at]], axis=0))
        hidden = silu_of_half(pre).astype(BF16)
        acc[...] += nt(hd[:, at], hidden)
        return carry

    lax.fori_loop(0, chunks, step, 0, unroll=True)
    agg[...] = acc[...].astype(BF16)
    swap = remote(agg, agg_o, 9, partner)
    swap.start()
    inner += mm(agg[...], pmix[...])
    swap.wait()
    inner = 0.5 * (inner + mm(agg_o[...], pmix[...]))
    upd[...] = silu_of_half(inner).astype(BF16)
    last = remote(upd, upd_o, 10, partner)
    last.start()
    kept = first + mm(upd[...], nout[...])
    last.wait()
    out[...] = (kept + mm(upd_o[...], nout_o[...])).astype(BF16)


def on_device(
    grid_field, band_points, block_ids, block_count, block_weight, embed_weight,
    edge_src, edge_dst, edge_in_weight, edge_out_weight, node_in_weight, node_out_weight,
):
    n = lax.axis_size("band")
    channels, points = grid_field.shape
    slots, nodes, block_len = block_weight.shape[1:]
    sub = points // block_len
    width = block_len // 2
    cols = embed_weight.shape[1]
    hid = 2 * cols
    edges = edge_src.shape[0] // 2
    bf = lambda *shape: pltpu.VMEM(shape, BF16)
    f32 = lambda *shape: pltpu.VMEM(shape, F32)
    return pl.pallas_call(
        functools.partial(layer_kernel, n),
        out_shape=jax.ShapeDtypeStruct((nodes, cols), BF16),
        in_specs=[SMEM] * 3 + [HBM] * 9, out_specs=VMEM,
        scratch_shapes=[
            bf(2 * sub + 1, channels, width), bf(nodes, slots * width),
            bf(2, channels, cols), bf(PAD, hid), bf(2, cols, hid), bf(2, hid, cols), bf(2, hid, cols),
            bf(cols, cols), bf(cols, cols),
            pltpu.VMEM((1, edges), jnp.int32), pltpu.VMEM((1, edges), jnp.int32),
            bf(hid, 2 * PAD), bf(PAD, cols), bf(hid, cols), bf(3 * nodes, edges), bf(nodes, edges),
            f32(PAD, nodes), f32(PAD, nodes), bf(3, PAD, nodes), bf(PAD, 2 * nodes),
            bf(PAD, edges), bf(PAD, edges), f32(nodes, hid),
            bf(nodes, hid), bf(nodes, hid), bf(nodes, cols), bf(nodes, cols),
            pltpu.SemaphoreType.DMA((slots,)), pltpu.SemaphoreType.DMA((sub,)), pltpu.SemaphoreType.DMA((7,)),
            pltpu.SemaphoreType.DMA((11,)), pltpu.SemaphoreType.DMA((11,)),
        ],
        compiler_params=pltpu.CompilerParams(vmem_limit_bytes=LARGE, collective_id=0, has_side_effects=True),
    )(
        block_ids, block_count, band_points, grid_field, block_weight.reshape(block_weight.shape[1:]),
        embed_weight, edge_out_weight, edge_in_weight, node_in_weight, node_out_weight,
        edge_src.reshape(1, -1), edge_dst.reshape(1, -1),
    )


def solution(mesh):
    return jax.shard_map(
        on_device,
        mesh=mesh,
        in_specs=(
            P(None, "band"), P("band"), P("band", None), P("band"),
            P("band", None, None, None), P(None, "ch"), P("band"), P("band"),
            P(None, None, "ch"), P("ch", None), P(None, None, "ch"), P("ch", None),
        ),
        out_specs=P("band", "ch"),
        check_vma=False,
    )
```

time: 69.5 us -> 54.4 us (0.78)
  the two profiles are of different devices: /device:TPU:33 before, /device:TPU:129 now
where the time goes in v1:
time: 54.4 us; the launch traced here: 54 us
  Pallas kernels  45 us (83%)
  local copies, waits for them, and re-layouts  7.74 us (14%)
  between operations  1.32 us (2%)
    pallas_call x1, Pallas kernels, on_device(): pl.pallas_call(functools.partial(layer_kernel, n), out_shape=jax.ShapeDty...  45 us
    unnamed x15, local copies, waits for them, and re-layouts  7.74 us

profile of v1, /device:TPU:129, one launch (start us, length us, event | category | flops | bytes accessed | tf_op | source)
XLA Modules:
  0.0 54.0 jit_solution(2381372406243951985)
XLA Ops:
  1.3 0.0 copy-start
  1.3 1.6 %copy-done = bf16[2,1024,512]{2,1,0:T(8,128)(2,1)S(1)} copy-done((bf16[2,1024,512]{2,1,0:T(8,128)(2,1)S(1)}, bf16[2,1024,512]{2,1,0:T(8,128)(2,1)}, u32[]{:S(2)}) %copy-start) | copy-done | bytes 2097176
  2.9 0.0 copy-start.1
  2.9 1.2 %copy-done.1 = bf16[512,1024]{1,0:T(8,128)(2,1)S(1)} copy-done((bf16[512,1024]{1,0:T(8,128)(2,1)S(1)}, bf16[512,1024]{1,0:T(8,128)(2,1)}, u32[]{:S(2)}) %copy-start.1) | copy-done | bytes 1048600
  4.1 0.0 copy-start.2
  4.1 1.2 %copy-done.2 = bf16[512,1024]{1,0:T(8,128)(2,1)S(1)} copy-done((bf16[512,1024]{1,0:T(8,128)(2,1)S(1)}, bf16[512,1024]{1,0:T(8,128)(2,1)}, u32[]{:S(2)}) %copy-start.2) | copy-done | bytes 1048600
  5.3 0.0 copy-start.3
  5.3 0.9 %copy-done.3 = bf16[100,512]{1,0:T(8,128)(2,1)S(1)} copy-done((bf16[100,512]{1,0:T(8,128)(2,1)S(1)}, bf16[100,512]{1,0:T(8,128)(2,1)}, u32[]{:S(2)}) %copy-start.3) | copy-done | bytes 102424
  6.2 0.0 copy-start.4
  6.2 0.7 %copy-done.4 = s32[5120]{0:T(1024)S(1)} copy-done((s32[5120]{0:T(1024)S(1)}, s32[5120]{0:T(1024)}, u32[]{:S(2)}) %copy-start.4) | copy-done | bytes 20504
  7.0 0.0 copy-start.5
  7.0 0.7 %copy-done.5 = s32[5120]{0:T(1024)S(1)} copy-done((s32[5120]{0:T(1024)S(1)}, s32[5120]{0:T(1024)}, u32[]{:S(2)}) %copy-start.5) | copy-done | bytes 20504
  7.7 0.0 copy-start.6
  7.7 0.7 %copy-done.6 = s32[1,16]{1,0:T(1,128)S(1)} copy-done((s32[1,16]{1,0:T(1,128)S(1)}, s32[1,16]{1,0:T(1,128)}, u32[]{:S(2)}) %copy-start.6) | copy-done | bytes 88
  8.3 45.0 %shard_map.118 = bf16[256,512]{1,0:T(8,128)(2,1)S(1)} custom-call(s32[1,16]{1,0:T(1,128)S(1)} %copy-done.6, s32[1]{0:T(128)S(6)} %copy.15.count, s32[1]{0:T(128)S(6)} %copy.14.live, bf16[100,16384]{1,0:T(8,128)(2,1)} %grid_h.1, bf16[16,256,512]{2,1,0:T(8,128)(2,1)} %bitcast.5, bf16[100,512]{1,0:T(8,128)(2,1)S(1)} %copy-done.3, ...), custom_call_target="tpu_custom_call" | custom-call | tf_op jit(solution)/shard_map/pallas_call | solution.py:235
  53.3 0.7 %copy.16 = bf16[256,512]{1,0:T(8,128)(2,1)} copy(bf16[256,512]{1,0:T(8,128)(2,1)S(1)} %shard_map.118) | data formatting | bytes 524288
Async XLA Ops:
  1.3 1.6 %copy-start = (bf16[2,1024,512]{2,1,0:T(8,128)(2,1)S(1)}, bf16[2,1024,512]{2,1,0:T(8,128)(2,1)}, u32[]{:S(2)}) copy-start(bf16[2,1024,512]{2,1,0:T(8,128)(2,1)} %win_h.1) | copy-start | bytes 6291460
  2.9 1.2 %copy-start.1 = (bf16[512,1024]{1,0:T(8,128)(2,1)S(1)}, bf16[512,1024]{1,0:T(8,128)(2,1)}, u32[]{:S(2)}) copy-start(bf16[512,1024]{1,0:T(8,128)(2,1)} %eo_h.1) | copy-start | bytes 3145732
  4.1 1.2 %copy-start.2 = (bf16[512,1024]{1,0:T(8,128)(2,1)S(1)}, bf16[512,1024]{1,0:T(8,128)(2,1)}, u32[]{:S(2)}) copy-start(bf16[512,1024]{1,0:T(8,128)(2,1)} %nout_h.1) | copy-start | bytes 3145732
  5.3 0.9 %copy-start.3 = (bf16[100,512]{1,0:T(8,128)(2,1)S(1)}, bf16[100,512]{1,0:T(8,128)(2,1)}, u32[]{:S(2)}) copy-start(bf16[100,512]{1,0:T(8,128)(2,1)} %emb_h.1) | copy-start | bytes 307204
  6.2 0.7 %copy-start.4 = (s32[5120]{0:T(1024)S(1)}, s32[5120]{0:T(1024)}, u32[]{:S(2)}) copy-start(s32[5120]{0:T(1024)} %param.18) | copy-start | bytes 61444
  7.0 0.7 %copy-start.5 = (s32[5120]{0:T(1024)S(1)}, s32[5120]{0:T(1024)}, u32[]{:S(2)}) copy-start(s32[5120]{0:T(1024)} %param.19) | copy-start | bytes 61444
  7.7 0.7 %copy-start.6 = (s32[1,16]{1,0:T(1,128)S(1)}, s32[1,16]{1,0:T(1,128)}, u32[]{:S(2)}) copy-start(s32[1,16]{1,0:T(1,128)} %ids.1) | copy-start | bytes 196

commit v2 on v1

v2 whole, which is shorter than its diff:
```python
import functools

import jax
import jax.numpy as jnp
from jax import lax
from jax.experimental import pallas as pl
from jax.experimental.pallas import tpu as pltpu
from jax.sharding import PartitionSpec as P

MESH = pl.DeviceIdType.MESH
F32 = jnp.float32
BF16 = jnp.bfloat16
VMEM = pl.BlockSpec(memory_space=pltpu.VMEM)
SMEM = pl.BlockSpec(memory_space=pltpu.SMEM)
HBM = pl.BlockSpec(memory_space=pltpu.HBM)
LARGE = 63 * 1024 * 1024
CHUNK = 512
PAD = 128
ROWS = 112


def nt(x, y):
    return lax.dot_general(x, y, (((1,), (1,)), ((), ())), preferred_element_type=F32)


def mm(x, y):
    return jnp.dot(x, y, preferred_element_type=F32)


def silu_of_half(v):
    return v + v * jnp.tanh(v)


def layer_kernel(
    n, ids, count, live, grid_h, w_h, emb_h, eo_h, win_h, nin_h, nout_h, src_h, dst_h, out,
    pool, wts, wt, emb, embp, eo, win, nin, nout, src, dst,
    mt, dmix, pmix, hs, hd, part, other, ext, near, gown, gath, acc, give, take, fin,
    wsem, gsem, lsem, send, recv,
):
    b = lax.axis_index("band")
    c = lax.axis_index("ch")
    slots, nodes, block_len = w_h.shape
    width = block_len // 2
    channels = grid_h.shape[0]
    sub = grid_h.shape[1] // block_len
    half = sub // 2
    cols = emb_h.shape[1]
    hid = 2 * cols
    mine_e = src.shape[1]
    chunks = mine_e // CHUNK
    mid = nodes // 2
    dead = 2 * sub
    up, down = jnp.minimum(b + 1, n - 1), jnp.maximum(b - 1, 0)
    has_up, has_down = b < n - 1, b > 0
    above, below, partner = (up, c), (down, c), (b, 1 - c)

    ext[...] = jnp.zeros_like(ext)
    barrier = pltpu.get_barrier_semaphore()

    @pl.when(has_up)
    def _():
        pl.semaphore_signal(barrier, inc=1, device_id=above, device_id_type=MESH)

    @pl.when(has_down)
    def _():
        pl.semaphore_signal(barrier, inc=1, device_id=below, device_id_type=MESH)

    pl.semaphore_signal(barrier, inc=1, device_id=partner, device_id_type=MESH)

    off = pl.multiple_of(c * width, width)
    gcopies = [
        pltpu.make_async_copy(
            grid_h.at[:, pl.ds(pl.multiple_of((2 * i + c) * width, width), width)], pool.at[half + i], gsem.at[i]
        )
        for i in range(sub)
    ]
    for one in gcopies[half:] + gcopies[:half]:
        one.start()
    wcopies = [
        pltpu.make_async_copy(w_h.at[k, :, pl.ds(off, width)], wts.at[:, pl.ds(k * width, width)], wsem.at[k])
        for k in range(slots)
    ]
    mine = pl.ds(pl.multiple_of(c * cols, cols), cols)
    theirs = pl.ds(pl.multiple_of((1 - c) * cols, cols), cols)
    near_n = pl.ds(pl.multiple_of(c * mid, mid), mid)
    far_n = pl.ds(pl.multiple_of((1 - c) * mid, mid), mid)
    edges = pl.ds(pl.multiple_of(c * mine_e, mine_e), mine_e)
    local = [
        pltpu.make_async_copy(x, y, lsem.at[i])
        for i, (x, y) in enumerate(
            [(emb_h, emb.at[c]), (win_h, win), (eo_h, eo.at[mine]), (nin_h, nin), (nout_h, nout.at[mine]),
             (src_h.at[:, edges], src), (dst_h.at[:, edges], dst)]
        )
    ]

    def remote(source, target, k, device):
        return pltpu.make_async_remote_copy(
            src_ref=source, dst_ref=target, send_sem=send.at[k], recv_sem=recv.at[k],
            device_id=device, device_id_type=MESH,
        )

    def neighbours(fwd, bwd):
        def end():
            @pl.when(has_up)
            def _():
                fwd.wait_send()
                bwd.wait_recv()

            @pl.when(has_down)
            def _():
                bwd.wait_send()
                fwd.wait_recv()

        return (lambda: pl.when(has_up)(fwd.start)), (lambda: pl.when(has_down)(bwd.start)), end

    halo_up, halo_down, halo_end = neighbours(
        remote(pool.at[pl.ds(sub, half)], pool.at[pl.ds(0, half)], 0, above),
        remote(pool.at[pl.ds(half, half)], pool.at[pl.ds(half + sub, half)], 1, below),
    )
    sent = pl.ds(0, ROWS)
    rows_up, rows_down, rows_end = neighbours(
        remote(ext.at[1, sent], ext.at[0, sent], 2, above), remote(ext.at[1, sent], ext.at[2, sent], 3, below)
    )
    weights = [
        remote(emb_h, emb.at[c], 4, partner), remote(eo_h, eo.at[mine], 5, partner),
        remote(nout_h, nout.at[mine], 6, partner),
    ]

    column = lax.broadcasted_iota(jnp.int32, (channels, width), 1) + c * width
    for one in gcopies:
        one.wait()
    for i in range(half, sub):
        block = pool[half + i]
        pool[half + i] = jnp.where(column < live[0] - i * block_len, block, jnp.zeros_like(block))
    pl.semaphore_wait(barrier, 1 + has_up.astype(jnp.int32) + has_down.astype(jnp.int32))
    halo_down()
    halo_up()
    for one in local + wcopies + weights:
        one.start()

    pool[dead] = jnp.zeros((channels, width), BF16)

    @pl.when(b == 0)
    def _():
        pool[0:half] = jnp.zeros((half, channels, width), BF16)

    @pl.when(b == n - 1)
    def _():
        pool[half + sub:dead] = jnp.zeros((half, channels, width), BF16)

    embp[...] = jnp.zeros_like(embp)
    acc[...] = jnp.zeros_like(acc)
    part[...] = jnp.zeros_like(part)
    for one in local + weights:
        one.wait()
    embp[0:channels, 0:cols] = emb[0]
    embp[0:channels, cols:hid] = emb[1]
    for i in range(2):
        mixed = mm(embp[...], win[i]) * 0.5
        mt[mine, i * PAD:(i + 1) * PAD] = mixed.T.astype(BF16)
    dmix[c] = (mm(embp[...], nin[0]) * 0.5).astype(BF16)
    pmix[c] = (mm(eo[...], nin[1]) * 0.5).astype(BF16)
    shares = [
        remote(mt.at[mine], mt.at[mine], 7, partner), remote(dmix.at[c], dmix.at[c], 8, partner),
        remote(pmix.at[c], pmix.at[c], 9, partner),
    ]
    for one in shares:
        one.start()

    def hot(i, carry):
        at = pl.ds(pl.multiple_of(i * CHUNK, CHUNK), CHUNK)
        s = src[:, at] - (b - 1) * nodes
        s = jnp.where(s < nodes, s, jnp.where(s < 2 * nodes, s + nodes, s - nodes))
        d = dst[:, at] - b * nodes
        hs[:, at] = jnp.where(lax.broadcasted_iota(jnp.int32, (3 * nodes, CHUNK), 0) == s, 1.0, 0.0).astype(BF16)
        hd[:, at] = jnp.where(lax.broadcasted_iota(jnp.int32, (nodes, CHUNK), 0) == d, 1.0, 0.0).astype(BF16)
        return carry

    lax.fori_loop(0, chunks, hot, 0)
    for one in wcopies:
        one.wait()
    for k in range(slots):
        at = slice(k * width, (k + 1) * width)
        wt[at, :] = wts[:, at].T
    for one in shares:
        one.wait()
    halo_end()

    picked = []
    for k in range(slots):
        rel = jnp.clip(ids[0, k] - b * sub + half, 0, dead - 1)
        picked.append(pool[jnp.where(k < count[0], rel, dead)])
    part[0:channels, :] = mm(jnp.concatenate(picked, axis=1), wt[...])
    swap = remote(part, other, 10, partner)
    swap.start()
    swap.wait_recv()
    own = (part[...] + other[...]).astype(BF16)
    ext[1] = own
    rows_up()
    rows_down()

    gath[PAD:, :] = mm(own, hd[...]).astype(BF16)
    gown[...] = mm(own, hs[2 * nodes:, :]).astype(BF16)
    rows = ext[1, :, near_n].astype(F32).T.astype(BF16)
    inner = [mm(rows, dmix[i]) for i in range(2)]
    first = mm(rows, embp[...]).astype(BF16)
    fin[...] = first
    swap.wait_send()
    rows_end()
    near[:, 0:nodes] = ext[0]
    near[:, nodes:] = ext[2]

    def pre_of(i):
        at = slice(i * CHUNK, (i + 1) * CHUNK)
        return mm(mt[...], gath[:, at])

    def edge_phase():
        gath[0:PAD, :] = (mm(near[...], hs[0:2 * nodes, :]) + gown[...].astype(F32)).astype(BF16)
        later = pre_of(0)
        for i in range(chunks):
            pre = later
            if i + 1 < chunks:
                later = pre_of(i + 1)
            hidden = silu_of_half(pre).astype(BF16)
            acc[...] += nt(hd[:, i * CHUNK:(i + 1) * CHUNK], hidden)

    edge_phase()

    give[...] = acc[far_n].astype(BF16)
    swap = remote(give, take, 11, partner)
    swap.start()
    swap.wait()
    total = (acc[near_n] + take[...].astype(F32)).astype(BF16)
    update = [silu_of_half(inner[i] + mm(total, pmix[i])).astype(BF16) for i in range(2)]
    update = jnp.concatenate(update, axis=1)
    fin[:, theirs] = (fin[:, theirs].astype(F32) + mm(update, nout[:, theirs])).astype(BF16)
    last = remote(fin.at[:, theirs], out.at[near_n], 12, partner)
    last.start()
    out[near_n] = (fin[:, mine].astype(F32) + mm(update, nout[:, mine])).astype(BF16)
    last.wait()


def on_device(
    grid_field, band_points, block_ids, block_count, block_weight, embed_weight,
    edge_src, edge_dst, edge_in_weight, edge_out_weight, node_in_weight, node_out_weight,
):
    n = lax.axis_size("band")
    channels, points = grid_field.shape
    slots, nodes, block_len = block_weight.shape[1:]
    sub = points // block_len
    width = block_len // 2
    cols = embed_weight.shape[1]
    hid = 2 * cols
    edges = edge_src.shape[0] // 2
    bf = lambda *shape: pltpu.VMEM(shape, BF16)
    f32 = lambda *shape: pltpu.VMEM(shape, F32)
    return pl.pallas_call(
        functools.partial(layer_kernel, n),
        out_shape=jax.ShapeDtypeStruct((nodes, cols), BF16),
        in_specs=[SMEM] * 3 + [HBM] * 9, out_specs=VMEM,
        scratch_shapes=[
            bf(2 * sub + 1, channels, width), bf(nodes, slots * width), bf(slots * width, nodes),
            bf(2, channels, cols), bf(PAD, hid), bf(hid, hid), bf(2, hid, cols), bf(2, hid, cols), bf(hid, hid),
            pltpu.VMEM((1, edges), jnp.int32), pltpu.VMEM((1, edges), jnp.int32),
            bf(hid, 2 * PAD), bf(2, PAD, cols), bf(2, hid, cols), bf(3 * nodes, edges), bf(nodes, edges),
            f32(PAD, nodes), f32(PAD, nodes), bf(3, PAD, nodes), bf(PAD, 2 * nodes),
            bf(PAD, edges), bf(2 * PAD, edges), f32(nodes, hid),
            bf(nodes // 2, hid), bf(nodes // 2, hid), bf(nodes // 2, hid),
            pltpu.SemaphoreType.DMA((slots,)), pltpu.SemaphoreType.DMA((sub,)), pltpu.SemaphoreType.DMA((7,)),
            pltpu.SemaphoreType.DMA((13,)), pltpu.SemaphoreType.DMA((13,)),
        ],
        compiler_params=pltpu.CompilerParams(vmem_limit_bytes=LARGE, collective_id=0, has_side_effects=True),
    )(
        block_ids, block_count, band_points, grid_field, block_weight.reshape(block_weight.shape[1:]),
        embed_weight, edge_out_weight, edge_in_weight, node_in_weight, node_out_weight,
        edge_src.reshape(1, -1), edge_dst.reshape(1, -1),
    )


def solution(mesh):
    return jax.shard_map(
        on_device,
        mesh=mesh,
        in_specs=(
            P(None, "band"), P("band"), P("band", None), P("band"),
            P("band", None, None, None), P(None, "ch"), P("band"), P("band"),
            P(None, None, "ch"), P("ch", None), P(None, None, "ch"), P("ch", None),
        ),
        out_specs=P("band", "ch"),
        check_vma=False,
    )
```

time: 54.4 us -> 46 us (0.85)
  local copies, waits for them, and re-layouts: 7.74 us -> 1.67 us
  Pallas kernels: 45 us -> 42.9 us
    unnamed x15 -> x1, local copies, waits for them, and re-layouts: 7.74 us -> 1.67 us
    pallas_call x1, Pallas kernels: 45 us -> 42.9 us  [on_device(): pl.pallas_call(functools.partial(layer_kernel, n), out_shape=jax.ShapeDty...]
where the time goes in v2:
time: 46 us; the launch traced here: 45.8 us
  Pallas kernels  42.9 us (93%)
  local copies, waits for them, and re-layouts  1.67 us (4%)
  between operations  1.3 us (3%)
    pallas_call x1, Pallas kernels, on_device(): pl.pallas_call(functools.partial(layer_kernel, n), out_shape=jax.ShapeDty...  42.9 us
    unnamed x1, local copies, waits for them, and re-layouts  1.67 us

profile of v2, /device:TPU:129, one launch (start us, length us, event | category | flops | bytes accessed | tf_op | source)
XLA Modules:
  0.0 45.8 jit_solution(5047082134800775632)
XLA Ops:
  1.3 42.9 %shard_map.118 = bf16[256,512]{1,0:T(8,128)(2,1)} custom-call(s32[1,16]{1,0:T(1,128)} %ids.1, s32[1]{0:T(128)S(6)} %copy.15.count, s32[1]{0:T(128)S(6)} %copy.14.live, bf16[100,16384]{1,0:T(8,128)(2,1)} %grid_h.1, bf16[16,256,512]{2,1,0:T(8,128)(2,1)} %bitcast.3, bf16[100,512]{1,0:T(8,128)(2,1)} %emb_h.1, bf16[512,1024]{1,0:T(8,128)(2,1)} %eo_h.1, ...), custom_call_target="tpu_custom_call" | custom-call | tf_op jit(solution)/shard_map/pallas_call | solution.py:257
  44.2 1.7 %copy.16 = bf16[256,512]{1,0:T(8,128)(2,1)} copy(bf16[256,512]{1,0:T(8,128)(2,1)} %shard_map.118) | data formatting | bytes 524288

commit v3 on v2

--- a/solution.py
+++ b/solution.py
@@ -13,7 +13,7 @@
 VMEM = pl.BlockSpec(memory_space=pltpu.VMEM)
 SMEM = pl.BlockSpec(memory_space=pltpu.SMEM)
 HBM = pl.BlockSpec(memory_space=pltpu.HBM)
-LARGE = 63 * 1024 * 1024
+LARGE = int(50 * 1024 * 1024)
 CHUNK = 512
 PAD = 128
 ROWS = 112
@@ -32,10 +32,10 @@
 
 
 def layer_kernel(
-    n, ids, count, live, grid_h, w_h, emb_h, eo_h, win_h, nin_h, nout_h, src_h, dst_h, out,
-    pool, wts, wt, emb, embp, eo, win, nin, nout, src, dst,
-    mt, dmix, pmix, hs, hd, part, other, ext, near, gown, gath, acc, give, take, fin,
-    wsem, gsem, lsem, send, recv,
+    n, count, live, ids_h, grid_h, w_h, emb_h, eo_h, win_h, nin_h, nout_h, src_h, dst_h, out,
+    ids, pool, wts, wt, emb, embp, eo, win, nin, nout, src, dst,
+    mt, mix, hs, hd, part, other, ext, near, gown, gath, acc, give, take, fin,
+    ssem, wsem, gsem, lsem, send, recv,
 ):
     b = lax.axis_index("band")
     c = lax.axis_index("ch")
@@ -70,16 +70,14 @@
     off = pl.multiple_of(c * width, width)
     gcopies = [
         pltpu.make_async_copy(
-            grid_h.at[:, pl.ds(pl.multiple_of((2 * i + c) * width, width), width)], pool.at[half + i], gsem.at[i]
+            grid_h.at[:, pl.ds(pl.multiple_of((2 * i + c) * width, width), width)], pool.at[half + i], gsem
         )
         for i in range(sub)
     ]
-    for one in gcopies[half:] + gcopies[:half]:
+    names = pltpu.make_async_copy(ids_h, ids, ssem)
+    for one in [names] + gcopies[half:] + gcopies[:half]:
         one.start()
-    wcopies = [
-        pltpu.make_async_copy(w_h.at[k, :, pl.ds(off, width)], wts.at[:, pl.ds(k * width, width)], wsem.at[k])
-        for k in range(slots)
-    ]
+    wcopy = pltpu.make_async_copy(w_h.at[:, :, pl.ds(off, width)], wts, wsem)
     mine = pl.ds(pl.multiple_of(c * cols, cols), cols)
     theirs = pl.ds(pl.multiple_of((1 - c) * cols, cols), cols)
     near_n = pl.ds(pl.multiple_of(c * mid, mid), mid)
@@ -127,15 +125,15 @@
     ]
 
     column = lax.broadcasted_iota(jnp.int32, (channels, width), 1) + c * width
-    for one in gcopies:
-        one.wait()
+    pltpu.make_async_copy(pool.at[pl.ds(half, sub)], pool.at[pl.ds(half, sub)], gsem).wait()
+    names.wait()
     for i in range(half, sub):
         block = pool[half + i]
         pool[half + i] = jnp.where(column < live[0] - i * block_len, block, jnp.zeros_like(block))
     pl.semaphore_wait(barrier, 1 + has_up.astype(jnp.int32) + has_down.astype(jnp.int32))
     halo_down()
     halo_up()
-    for one in local + wcopies + weights:
+    for one in local + [wcopy] + weights:
         one.start()
 
     pool[dead] = jnp.zeros((channels, width), BF16)
@@ -158,11 +156,10 @@
     for i in range(2):
         mixed = mm(embp[...], win[i]) * 0.5
         mt[mine, i * PAD:(i + 1) * PAD] = mixed.T.astype(BF16)
-    dmix[c] = (mm(embp[...], nin[0]) * 0.5).astype(BF16)
-    pmix[c] = (mm(eo[...], nin[1]) * 0.5).astype(BF16)
+    mix[c, hid:] = (mm(embp[...], nin[0]) * 0.5).astype(BF16)
+    mix[c, 0:hid] = (mm(eo[...], nin[1]) * 0.5).astype(BF16)
     shares = [
-        remote(mt.at[mine], mt.at[mine], 7, partner), remote(dmix.at[c], dmix.at[c], 8, partner),
-        remote(pmix.at[c], pmix.at[c], 9, partner),
+        remote(mt.at[mine], mt.at[mine], 7, partner), remote(mix.at[c], mix.at[c], 8, partner),
     ]
     for one in shares:
         one.start()
@@ -177,11 +174,9 @@
         return carry
 
     lax.fori_loop(0, chunks, hot, 0)
-    for one in wcopies:
-        one.wait()
+    wcopy.wait()
     for k in range(slots):
-        at = slice(k * width, (k + 1) * width)
-        wt[at, :] = wts[:, at].T
+        wt[k * width:(k + 1) * width, :] = wts[k].T
     for one in shares:
         one.wait()
     halo_end()
@@ -191,7 +186,7 @@
         rel = jnp.clip(ids[0, k] - b * sub + half, 0, dead - 1)
         picked.append(pool[jnp.where(k < count[0], rel, dead)])
     part[0:channels, :] = mm(jnp.concatenate(picked, axis=1), wt[...])
-    swap = remote(part, other, 10, partner)
+    swap = remote(part, other, 9, partner)
     swap.start()
     swap.wait_recv()
     own = (part[...] + other[...]).astype(BF16)
@@ -202,7 +197,7 @@
     gath[PAD:, :] = mm(own, hd[...]).astype(BF16)
     gown[...] = mm(own, hs[2 * nodes:, :]).astype(BF16)
     rows = ext[1, :, near_n].astype(F32).T.astype(BF16)
-    inner = [mm(rows, dmix[i]) for i in range(2)]
+    inner = [mm(rows, mix[i, hid:]) for i in range(2)]
     first = mm(rows, embp[...]).astype(BF16)
     fin[...] = first
     swap.wait_send()
@@ -227,14 +222,14 @@
     edge_phase()
 
     give[...] = acc[far_n].astype(BF16)
-    swap = remote(give, take, 11, partner)
+    swap = remote(give, take, 10, partner)
     swap.start()
     swap.wait()
     total = (acc[near_n] + take[...].astype(F32)).astype(BF16)
-    update = [silu_of_half(inner[i] + mm(total, pmix[i])).astype(BF16) for i in range(2)]
+    update = [silu_of_half(inner[i] + mm(total, mix[i, 0:hid])).astype(BF16) for i in range(2)]
     update = jnp.concatenate(update, axis=1)
     fin[:, theirs] = (fin[:, theirs].astype(F32) + mm(update, nout[:, theirs])).astype(BF16)
-    last = remote(fin.at[:, theirs], out.at[near_n], 12, partner)
+    last = remote(fin.at[:, theirs], out.at[near_n], 11, partner)
     last.start()
     out[near_n] = (fin[:, mine].astype(F32) + mm(update, nout[:, mine])).astype(BF16)
     last.wait()
@@ -256,24 +251,27 @@
     f32 = lambda *shape: pltpu.VMEM(shape, F32)
     return pl.pallas_call(
         functools.partial(layer_kernel, n),
-        out_shape=jax.ShapeDtypeStruct((nodes, cols), BF16),
-        in_specs=[SMEM] * 3 + [HBM] * 9, out_specs=VMEM,
+        out_shape=pltpu.VMEM((nodes, cols), BF16),
+        in_specs=[SMEM] * 2 + [HBM] * 10, out_specs=VMEM,
         scratch_shapes=[
-            bf(2 * sub + 1, channels, width), bf(nodes, slots * width), bf(slots * width, nodes),
+            pltpu.SMEM((1, slots), jnp.int32),
+            bf(2 * sub + 1, channels, width), bf(slots, nodes, width), bf(slots * width, nodes),
             bf(2, channels, cols), bf(PAD, hid), bf(hid, hid), bf(2, hid, cols), bf(2, hid, cols), bf(hid, hid),
             pltpu.VMEM((1, edges), jnp.int32), pltpu.VMEM((1, edges), jnp.int32),
-            bf(hid, 2 * PAD), bf(2, PAD, cols), bf(2, hid, cols), bf(3 * nodes, edges), bf(nodes, edges),
+            bf(hid, 2 * PAD), bf(2, hid + PAD, cols), bf(3 * nodes, edges), bf(nodes, edges),
             f32(PAD, nodes), f32(PAD, nodes), bf(3, PAD, nodes), bf(PAD, 2 * nodes),
             bf(PAD, edges), bf(2 * PAD, edges), f32(nodes, hid),
             bf(nodes // 2, hid), bf(nodes // 2, hid), bf(nodes // 2, hid),
-            pltpu.SemaphoreType.DMA((slots,)), pltpu.SemaphoreType.DMA((sub,)), pltpu.SemaphoreType.DMA((7,)),
-            pltpu.SemaphoreType.DMA((13,)), pltpu.SemaphoreType.DMA((13,)),
+            pltpu.SemaphoreType.DMA, pltpu.SemaphoreType.DMA, pltpu.SemaphoreType.DMA, pltpu.SemaphoreType.DMA((7,)),
+            pltpu.SemaphoreType.DMA((12,)), pltpu.SemaphoreType.DMA((12,)),
         ],
         compiler_params=pltpu.CompilerParams(vmem_limit_bytes=LARGE, collective_id=0, has_side_effects=True),
     )(
-        block_ids, block_count, band_points, grid_field, block_weight.reshape(block_weight.shape[1:]),
-        embed_weight, edge_out_weight, edge_in_weight, node_in_weight, node_out_weight,
-        edge_src.reshape(1, -1), edge_dst.reshape(1, -1),
+        block_count, band_points, *[pltpu.with_memory_space_constraint(x, pltpu.HBM) for x in (
+            block_ids, grid_field, block_weight.reshape(block_weight.shape[1:]),
+            embed_weight, edge_out_weight, edge_in_weight, node_in_weight, node_out_weight,
+            edge_src.reshape(1, -1), edge_dst.reshape(1, -1),
+        )],
     )
 
 

time: 46 us -> 43.3 us (0.941)
  Pallas kernels: 42.9 us -> 41.1 us
  local copies, waits for them, and re-layouts: 1.67 us -> 0.71 us
    pallas_call x1, Pallas kernels: 42.9 us -> 41.1 us  [on_device(): pl.pallas_call(functools.partial(layer_kernel, n), out_shape=pltpu.VMEM((...]
    unnamed x1, local copies, waits for them, and re-layouts: 1.67 us -> 0.71 us
where the time goes in v3:
time: 43.3 us; the launch traced here: 43.1 us
  Pallas kernels  41.1 us (95%)
  between operations  1.3 us (3%)
  local copies, waits for them, and re-layouts  0.71 us (2%)
    pallas_call x1, Pallas kernels, on_device(): pl.pallas_call(functools.partial(layer_kernel, n), out_shape=pltpu.VMEM((...  41.1 us

profile of v3, /device:TPU:129, one launch (start us, length us, event | category | flops | bytes accessed | tf_op | source)
XLA Modules:
  0.0 43.1 jit_solution(12497525492042926422)
XLA Ops:
  1.3 41.1 %shard_map.118 = bf16[256,512]{1,0:T(8,128)(2,1)S(1)} custom-call(s32[1]{0:T(128)S(6)} %copy.16.count, s32[1]{0:T(128)S(6)} %copy.15.live, s32[1,16]{1,0:T(1,128)} %ids_h.1, bf16[100,16384]{1,0:T(8,128)(2,1)} %grid_h.1, bf16[16,256,512]{2,1,0:T(8,128)(2,1)} %bitcast.3, bf16[100,512]{1,0:T(8,128)(2,1)} %emb_h.1, bf16[512,1024]{1,0:T(8,128)(2,1)} %eo_h.1, ...), custom_call_target="tpu_custom_call" | custom-call | tf_op jit(solution)/shard_map/pallas_call | solution.py:252
  42.4 0.7 %copy.14 = bf16[256,512]{1,0:T(8,128)(2,1)} copy(bf16[256,512]{1,0:T(8,128)(2,1)S(1)} %shard_map.118) | data formatting | bytes 524288

commit v4 on v3

--- a/solution.py
+++ b/solution.py
@@ -17,6 +17,7 @@
 CHUNK = 512
 PAD = 128
 ROWS = 112
+TILE = 16
 
 
 def nt(x, y):
@@ -33,7 +34,7 @@
 
 def layer_kernel(
     n, count, live, ids_h, grid_h, w_h, emb_h, eo_h, win_h, nin_h, nout_h, src_h, dst_h, out,
-    ids, pool, wts, wt, emb, embp, eo, win, nin, nout, src, dst,
+    ids, raw, pool, wts, wt, emb, embp, eo, win, nin, nout, src, dst,
     mt, mix, hs, hd, part, other, ext, near, gown, gath, acc, give, take, fin,
     ssem, wsem, gsem, lsem, send, recv,
 ):
@@ -49,7 +50,10 @@
     mine_e = src.shape[1]
     chunks = mine_e // CHUNK
     mid = nodes // 2
-    dead = 2 * sub
+    tall = channels // TILE
+    tail = channels % TILE
+    group = TILE // tail
+    quarter = (tall * half) + half // group
     up, down = jnp.minimum(b + 1, n - 1), jnp.maximum(b - 1, 0)
     has_up, has_down = b < n - 1, b > 0
     above, below, partner = (up, c), (down, c), (b, 1 - c)
@@ -70,7 +74,7 @@
     off = pl.multiple_of(c * width, width)
     gcopies = [
         pltpu.make_async_copy(
-            grid_h.at[:, pl.ds(pl.multiple_of((2 * i + c) * width, width), width)], pool.at[half + i], gsem
+            grid_h.at[:, pl.ds(pl.multiple_of((2 * i + c) * width, width), width)], raw.at[i], gsem
         )
         for i in range(sub)
     ]
@@ -112,8 +116,8 @@
         return (lambda: pl.when(has_up)(fwd.start)), (lambda: pl.when(has_down)(bwd.start)), end
 
     halo_up, halo_down, halo_end = neighbours(
-        remote(pool.at[pl.ds(sub, half)], pool.at[pl.ds(0, half)], 0, above),
-        remote(pool.at[pl.ds(half, half)], pool.at[pl.ds(half + sub, half)], 1, below),
+        remote(pool.at[pl.ds(2 * quarter, quarter)], pool.at[pl.ds(0, quarter)], 0, above),
+        remote(pool.at[pl.ds(quarter, quarter)], pool.at[pl.ds(3 * quarter, quarter)], 1, below),
     )
     sent = pl.ds(0, ROWS)
     rows_up, rows_down, rows_end = neighbours(
@@ -125,26 +129,35 @@
     ]
 
     column = lax.broadcasted_iota(jnp.int32, (channels, width), 1) + c * width
-    pltpu.make_async_copy(pool.at[pl.ds(half, sub)], pool.at[pl.ds(half, sub)], gsem).wait()
+    pltpu.make_async_copy(raw, raw, gsem).wait()
     names.wait()
-    for i in range(half, sub):
-        block = pool[half + i]
-        pool[half + i] = jnp.where(column < live[0] - i * block_len, block, jnp.zeros_like(block))
+    for i in range(0, sub, group):
+        ends = []
+        base, first_of = (1 + i // half) * quarter, i % half
+        for j in range(group):
+            block = raw[i + j]
+            if i >= half:
+                block = jnp.where(column < live[0] - (i + j) * block_len, block, jnp.zeros_like(block))
+            for t in range(tall):
+                pool[base + (first_of + j) * tall + t] = block[t * TILE:(t + 1) * TILE]
+            ends.append(block[tall * TILE:].astype(F32))
+        pool[base + tall * half + first_of // group] = jnp.concatenate(ends, axis=0).astype(BF16)
     pl.semaphore_wait(barrier, 1 + has_up.astype(jnp.int32) + has_down.astype(jnp.int32))
     halo_down()
     halo_up()
     for one in local + [wcopy] + weights:
         one.start()
 
-    pool[dead] = jnp.zeros((channels, width), BF16)
+    blank = jnp.zeros((quarter,) + pool.shape[1:], BF16)
+    pool[4 * quarter:] = blank
 
     @pl.when(b == 0)
     def _():
-        pool[0:half] = jnp.zeros((half, channels, width), BF16)
+        pool[0:quarter] = blank
 
     @pl.when(b == n - 1)
     def _():
-        pool[half + sub:dead] = jnp.zeros((half, channels, width), BF16)
+        pool[3 * quarter:4 * quarter] = blank
 
     embp[...] = jnp.zeros_like(embp)
     acc[...] = jnp.zeros_like(acc)
@@ -182,10 +195,20 @@
     halo_end()
 
     picked = []
+    line = lax.broadcasted_iota(jnp.int32, (TILE, width), 0)
     for k in range(slots):
-        rel = jnp.clip(ids[0, k] - b * sub + half, 0, dead - 1)
-        picked.append(pool[jnp.where(k < count[0], rel, dead)])
-    part[0:channels, :] = mm(jnp.concatenate(picked, axis=1), wt[...])
+        rel = jnp.clip(ids[0, k] - b * sub + half, 0, 2 * sub - 1)
+        part_of, i = rel // half, rel % half
+        base = jnp.where(k < count[0], part_of, 4) * quarter
+        low = i % group * tail
+        ends = pool[base + tall * half + i // group]
+        ends = jnp.where((line >= low) & (line < low + tail), ends, jnp.zeros_like(ends))
+        tiles = [pool[base + i * tall + t] for t in range(tall)]
+        picked.append(jnp.concatenate(tiles + [ends], axis=0))
+    mixed = mm(jnp.concatenate(picked, axis=1), wt[...])
+    top = tall * TILE
+    part[0:top, :] = mixed[:top]
+    part[top:channels, :] = sum(mixed[top + j * tail:top + (j + 1) * tail] for j in range(group))
     swap = remote(part, other, 9, partner)
     swap.start()
     swap.wait_recv()
@@ -255,7 +278,7 @@
         in_specs=[SMEM] * 2 + [HBM] * 10, out_specs=VMEM,
         scratch_shapes=[
             pltpu.SMEM((1, slots), jnp.int32),
-            bf(2 * sub + 1, channels, width), bf(slots, nodes, width), bf(slots * width, nodes),
+            bf(sub, channels, width), bf(5 * channels * sub // 2 // TILE, TILE, width), bf(slots, nodes, width), bf(slots * width, nodes),
             bf(2, channels, cols), bf(PAD, hid), bf(hid, hid), bf(2, hid, cols), bf(2, hid, cols), bf(hid, hid),
             pltpu.VMEM((1, edges), jnp.int32), pltpu.VMEM((1, edges), jnp.int32),
             bf(hid, 2 * PAD), bf(2, hid + PAD, cols), bf(3 * nodes, edges), bf(nodes, edges),

time: 43.3 us -> 42.6 us (0.984)
  Pallas kernels: 41.1 us -> 40.4 us
    pallas_call x1, Pallas kernels: 41.1 us -> 40.4 us  [on_device(): pl.pallas_call(functools.partial(layer_kernel, n), out_shape=pltpu.VMEM((...]
where the time goes in v4:
time: 42.6 us; the launch traced here: 42.4 us
  Pallas kernels  40.4 us (95%)
  between operations  1.3 us (3%)
  local copies, waits for them, and re-layouts  0.71 us (2%)
    pallas_call x1, Pallas kernels, on_device(): pl.pallas_call(functools.partial(layer_kernel, n), out_shape=pltpu.VMEM((...  40.4 us

profile of v4, /device:TPU:129, one launch (start us, length us, event | category | flops | bytes accessed | tf_op | source)
XLA Modules:
  0.0 42.4 jit_solution(601478184027909544)
XLA Ops:
  1.3 40.4 %shard_map.118 = bf16[256,512]{1,0:T(8,128)(2,1)S(1)} custom-call(s32[1]{0:T(128)S(6)} %copy.16.count, s32[1]{0:T(128)S(6)} %copy.15.live, s32[1,16]{1,0:T(1,128)} %ids_h.1, bf16[100,16384]{1,0:T(8,128)(2,1)} %grid_h.1, bf16[16,256,512]{2,1,0:T(8,128)(2,1)} %bitcast.3, bf16[100,512]{1,0:T(8,128)(2,1)} %emb_h.1, bf16[512,1024]{1,0:T(8,128)(2,1)} %eo_h.1, ...), custom_call_target="tpu_custom_call" | custom-call | tf_op jit(solution)/shard_map/pallas_call | solution.py:275
  41.7 0.7 %copy.14 = bf16[256,512]{1,0:T(8,128)(2,1)} copy(bf16[256,512]{1,0:T(8,128)(2,1)S(1)} %shard_map.118) | data formatting | bytes 524288

commit v5 on v4

--- a/solution.py
+++ b/solution.py
@@ -35,7 +35,7 @@
 def layer_kernel(
     n, count, live, ids_h, grid_h, w_h, emb_h, eo_h, win_h, nin_h, nout_h, src_h, dst_h, out,
     ids, raw, pool, wts, wt, emb, embp, eo, win, nin, nout, src, dst,
-    mt, mix, hs, hd, part, other, ext, near, gown, gath, acc, give, take, fin,
+    mt, mix, hs, hd, part, other, ext, gown, gath, acc, give, take, fin,
     ssem, wsem, gsem, lsem, send, recv,
 ):
     b = lax.axis_index("band")
@@ -102,25 +102,26 @@
         )
 
     def neighbours(fwd, bwd):
-        def end():
+        def end_up():
             @pl.when(has_up)
             def _():
                 fwd.wait_send()
                 bwd.wait_recv()
 
+        def end_down():
             @pl.when(has_down)
             def _():
                 bwd.wait_send()
                 fwd.wait_recv()
 
-        return (lambda: pl.when(has_up)(fwd.start)), (lambda: pl.when(has_down)(bwd.start)), end
-
-    halo_up, halo_down, halo_end = neighbours(
+        return (lambda: pl.when(has_up)(fwd.start)), (lambda: pl.when(has_down)(bwd.start)), end_up, end_down
+
+    halo_up, halo_down, halo_end_up, halo_end_down = neighbours(
         remote(pool.at[pl.ds(2 * quarter, quarter)], pool.at[pl.ds(0, quarter)], 0, above),
         remote(pool.at[pl.ds(quarter, quarter)], pool.at[pl.ds(3 * quarter, quarter)], 1, below),
     )
     sent = pl.ds(0, ROWS)
-    rows_up, rows_down, rows_end = neighbours(
+    rows_up, rows_down, rows_end_up, rows_end_down = neighbours(
         remote(ext.at[1, sent], ext.at[0, sent], 2, above), remote(ext.at[1, sent], ext.at[2, sent], 3, below)
     )
     weights = [
@@ -192,7 +193,8 @@
         wt[k * width:(k + 1) * width, :] = wts[k].T
     for one in shares:
         one.wait()
-    halo_end()
+    halo_end_up()
+    halo_end_down()
 
     picked = []
     line = lax.broadcasted_iota(jnp.int32, (TILE, width), 0)
@@ -224,16 +226,16 @@
     first = mm(rows, embp[...]).astype(BF16)
     fin[...] = first
     swap.wait_send()
-    rows_end()
-    near[:, 0:nodes] = ext[0]
-    near[:, nodes:] = ext[2]
+    rows_end_up()
+    gown[...] = (gown[...].astype(F32) + mm(ext[2], hs[nodes:2 * nodes, :])).astype(BF16)
+    rows_end_down()
 
     def pre_of(i):
         at = slice(i * CHUNK, (i + 1) * CHUNK)
         return mm(mt[...], gath[:, at])
 
     def edge_phase():
-        gath[0:PAD, :] = (mm(near[...], hs[0:2 * nodes, :]) + gown[...].astype(F32)).astype(BF16)
+        gath[0:PAD, :] = (mm(ext[0], hs[0:nodes, :]) + gown[...].astype(F32)).astype(BF16)
         later = pre_of(0)
         for i in range(chunks):
             pre = later
@@ -282,7 +284,7 @@
             bf(2, channels, cols), bf(PAD, hid), bf(hid, hid), bf(2, hid, cols), bf(2, hid, cols), bf(hid, hid),
             pltpu.VMEM((1, edges), jnp.int32), pltpu.VMEM((1, edges), jnp.int32),
             bf(hid, 2 * PAD), bf(2, hid + PAD, cols), bf(3 * nodes, edges), bf(nodes, edges),
-            f32(PAD, nodes), f32(PAD, nodes), bf(3, PAD, nodes), bf(PAD, 2 * nodes),
+            f32(PAD, nodes), f32(PAD, nodes), bf(3, PAD, nodes),
             bf(PAD, edges), bf(2 * PAD, edges), f32(nodes, hid),
             bf(nodes // 2, hid), bf(nodes // 2, hid), bf(nodes // 2, hid),
             pltpu.SemaphoreType.DMA, pltpu.SemaphoreType.DMA, pltpu.SemaphoreType.DMA, pltpu.SemaphoreType.DMA((7,)),

time: 42.6 us -> 42.4 us (level)
  no operation moved by 1% of the time
where the time goes in v5:
time: 42.4 us; the launch traced here: 42.2 us
  Pallas kernels  40.2 us (95%)
  between operations  1.3 us (3%)
  local copies, waits for them, and re-layouts  0.71 us (2%)
    pallas_call x1, Pallas kernels, on_device(): pl.pallas_call(functools.partial(layer_kernel, n), out_shape=pltpu.VMEM((...  40.2 us

profile of v5, /device:TPU:129, one launch (start us, length us, event | category | flops | bytes accessed | tf_op | source)
XLA Modules:
  0.0 42.2 jit_solution(11220629405955205262)
XLA Ops:
  1.3 40.2 %shard_map.118 = bf16[256,512]{1,0:T(8,128)(2,1)S(1)} custom-call(s32[1]{0:T(128)S(6)} %copy.16.count, s32[1]{0:T(128)S(6)} %copy.15.live, s32[1,16]{1,0:T(1,128)} %ids_h.1, bf16[100,16384]{1,0:T(8,128)(2,1)} %grid_h.1, bf16[16,256,512]{2,1,0:T(8,128)(2,1)} %bitcast.3, bf16[100,512]{1,0:T(8,128)(2,1)} %emb_h.1, bf16[512,1024]{1,0:T(8,128)(2,1)} %eo_h.1, ...), custom_call_target="tpu_custom_call" | custom-call | tf_op jit(solution)/shard_map/pallas_call | solution.py:277
  41.5 0.7 %copy.14 = bf16[256,512]{1,0:T(8,128)(2,1)} copy(bf16[256,512]{1,0:T(8,128)(2,1)S(1)} %shard_map.118) | data formatting | bytes 524288

commit v6 on v5

--- a/solution.py
+++ b/solution.py
@@ -16,7 +16,7 @@
 LARGE = int(50 * 1024 * 1024)
 CHUNK = 512
 PAD = 128
-ROWS = 112
+ROWS = 104
 TILE = 16
 
 
@@ -102,26 +102,21 @@
         )
 
     def neighbours(fwd, bwd):
-        def end_up():
-            @pl.when(has_up)
-            def _():
-                fwd.wait_send()
-                bwd.wait_recv()
-
-        def end_down():
-            @pl.when(has_down)
-            def _():
-                bwd.wait_send()
-                fwd.wait_recv()
-
-        return (lambda: pl.when(has_up)(fwd.start)), (lambda: pl.when(has_down)(bwd.start)), end_up, end_down
-
-    halo_up, halo_down, halo_end_up, halo_end_down = neighbours(
+        def sends():
+            pl.when(has_up)(fwd.wait_send)
+            pl.when(has_down)(bwd.wait_send)
+
+        return (
+            lambda: pl.when(has_up)(fwd.start), lambda: pl.when(has_down)(bwd.start),
+            lambda: pl.when(has_up)(bwd.wait_recv), lambda: pl.when(has_down)(fwd.wait_recv), sends,
+        )
+
+    halo_up, halo_down, halo_end_up, halo_end_down, halo_sends = neighbours(
         remote(pool.at[pl.ds(2 * quarter, quarter)], pool.at[pl.ds(0, quarter)], 0, above),
         remote(pool.at[pl.ds(quarter, quarter)], pool.at[pl.ds(3 * quarter, quarter)], 1, below),
     )
     sent = pl.ds(0, ROWS)
-    rows_up, rows_down, rows_end_up, rows_end_down = neighbours(
+    rows_up, rows_down, rows_end_up, rows_end_down, rows_sends = neighbours(
         remote(ext.at[1, sent], ext.at[0, sent], 2, above), remote(ext.at[1, sent], ext.at[2, sent], 3, below)
     )
     weights = [
@@ -163,6 +158,7 @@
     embp[...] = jnp.zeros_like(embp)
     acc[...] = jnp.zeros_like(acc)
     part[...] = jnp.zeros_like(part)
+    other[ROWS:] = jnp.zeros((PAD - ROWS, nodes), F32)
     for one in local + weights:
         one.wait()
     embp[0:channels, 0:cols] = emb[0]
@@ -211,7 +207,7 @@
     top = tall * TILE
     part[0:top, :] = mixed[:top]
     part[top:channels, :] = sum(mixed[top + j * tail:top + (j + 1) * tail] for j in range(group))
-    swap = remote(part, other, 9, partner)
+    swap = remote(part.at[sent], other.at[sent], 9, partner)
     swap.start()
     swap.wait_recv()
     own = (part[...] + other[...]).astype(BF16)
@@ -225,7 +221,6 @@
     inner = [mm(rows, mix[i, hid:]) for i in range(2)]
     first = mm(rows, embp[...]).astype(BF16)
     fin[...] = first
-    swap.wait_send()
     rows_end_up()
     gown[...] = (gown[...].astype(F32) + mm(ext[2], hs[nodes:2 * nodes, :])).astype(BF16)
     rows_end_down()
@@ -247,9 +242,12 @@
     edge_phase()
 
     give[...] = acc[far_n].astype(BF16)
-    swap = remote(give, take, 10, partner)
-    swap.start()
-    swap.wait()
+    trade = remote(give, take, 10, partner)
+    trade.start()
+    swap.wait_send()
+    halo_sends()
+    rows_sends()
+    trade.wait()
     total = (acc[near_n] + take[...].astype(F32)).astype(BF16)
     update = [silu_of_half(inner[i] + mm(total, mix[i, 0:hid])).astype(BF16) for i in range(2)]
     update = jnp.concatenate(update, axis=1)

time: 42.4 us -> 42.3 us (level)
  no operation moved by 1% of the time
where the time goes in v6:
time: 42.3 us; the launch traced here: 42.1 us
  Pallas kernels  40.1 us (95%)
  between operations  1.3 us (3%)
  local copies, waits for them, and re-layouts  0.71 us (2%)
    pallas_call x1, Pallas kernels, on_device(): pl.pallas_call(functools.partial(layer_kernel, n), out_shape=pltpu.VMEM((...  40.1 us

profile of v6, /device:TPU:129, one launch (start us, length us, event | category | flops | bytes accessed | tf_op | source)
XLA Modules:
  0.0 42.1 jit_solution(12125018580378988260)
XLA Ops:
  1.3 40.1 %shard_map.118 = bf16[256,512]{1,0:T(8,128)(2,1)S(1)} custom-call(s32[1]{0:T(128)S(6)} %copy.16.count, s32[1]{0:T(128)S(6)} %copy.15.live, s32[1,16]{1,0:T(1,128)} %ids_h.1, bf16[100,16384]{1,0:T(8,128)(2,1)} %grid_h.1, bf16[16,256,512]{2,1,0:T(8,128)(2,1)} %bitcast.3, bf16[100,512]{1,0:T(8,128)(2,1)} %emb_h.1, bf16[512,1024]{1,0:T(8,128)(2,1)} %eo_h.1, ...), custom_call_target="tpu_custom_call" | custom-call | tf_op jit(solution)/shard_map/pallas_call | solution.py:275
  41.4 0.7 %copy.14 = bf16[256,512]{1,0:T(8,128)(2,1)} copy(bf16[256,512]{1,0:T(8,128)(2,1)S(1)} %shard_map.118) | data formatting | bytes 524288

commit v7 on v6

--- a/solution.py
+++ b/solution.py
@@ -58,7 +58,6 @@
     has_up, has_down = b < n - 1, b > 0
     above, below, partner = (up, c), (down, c), (b, 1 - c)
 
-    ext[...] = jnp.zeros_like(ext)
     barrier = pltpu.get_barrier_semaphore()
 
     @pl.when(has_up)
@@ -150,14 +149,17 @@
     @pl.when(b == 0)
     def _():
         pool[0:quarter] = blank
+        ext[0, 0:ROWS] = jnp.zeros((ROWS, nodes), BF16)
 
     @pl.when(b == n - 1)
     def _():
         pool[3 * quarter:4 * quarter] = blank
+        ext[2, 0:ROWS] = jnp.zeros((ROWS, nodes), BF16)
 
     embp[...] = jnp.zeros_like(embp)
     acc[...] = jnp.zeros_like(acc)
     part[...] = jnp.zeros_like(part)
+    ext[:, ROWS:] = jnp.zeros((3, PAD - ROWS, nodes), BF16)
     other[ROWS:] = jnp.zeros((PAD - ROWS, nodes), F32)
     for one in local + weights:
         one.wait()

time: 42.3 us -> 42.3 us (level)
  no operation moved by 1% of the time
where the time goes in v7:
time: 42.3 us; the launch traced here: 42.1 us
  Pallas kernels  40.1 us (95%)
  between operations  1.3 us (3%)
  local copies, waits for them, and re-layouts  0.71 us (2%)
    pallas_call x1, Pallas kernels, on_device(): pl.pallas_call(functools.partial(layer_kernel, n), out_shape=pltpu.VMEM((...  40.1 us

profile of v7, /device:TPU:129, one launch (start us, length us, event | category | flops | bytes accessed | tf_op | source)
XLA Modules:
  0.0 42.1 jit_solution(1739788756435167261)
XLA Ops:
  1.3 40.1 %shard_map.118 = bf16[256,512]{1,0:T(8,128)(2,1)S(1)} custom-call(s32[1]{0:T(128)S(6)} %copy.16.count, s32[1]{0:T(128)S(6)} %copy.15.live, s32[1,16]{1,0:T(1,128)} %ids_h.1, bf16[100,16384]{1,0:T(8,128)(2,1)} %grid_h.1, bf16[16,256,512]{2,1,0:T(8,128)(2,1)} %bitcast.3, bf16[100,512]{1,0:T(8,128)(2,1)} %emb_h.1, bf16[512,1024]{1,0:T(8,128)(2,1)} %eo_h.1, ...), custom_call_target="tpu_custom_call" | custom-call | tf_op jit(solution)/shard_map/pallas_call | solution.py:277
  41.4 0.7 %copy.14 = bf16[256,512]{1,0:T(8,128)(2,1)} copy(bf16[256,512]{1,0:T(8,128)(2,1)S(1)} %shard_map.118) | data formatting | bytes 524288
